TPU v7x, 32 devices: a whole 2x2x4 slice. The times are simulated.
32 devices in a mesh: doc: 2 (over x), seq: 16 (over z, y, core).
Axes of the slice: x: 2, y: 2, z: 4, core: 2. Of those that a mesh axis runs over, the one named last changes fastest.
Arguments:
- queries: bfloat16 [4096, 1792], P(('doc', 'seq')), parts along dimension 0, may hold values from -5 to 5
- keys: bfloat16 [4096, 256], P(('doc', 'seq')), parts along dimension 0, may hold values from -5 to 5
- values: bfloat16 [4096, 256], P(('doc', 'seq')), parts along dimension 0, may hold values from -6 to 6
- doc_length: int32 [2], P('doc'), parts along dimension 0, may hold values from 1024 to 2048
- sink_pos: int32 [8], P('doc'), parts along dimension 0, may hold values from 0 to 127, as said below
Outputs:
- attended: bfloat16 [4096, 1792], P(('doc', 'seq')), parts along dimension 0
- row_lse: float32 [14, 4096], P(None, ('doc', 'seq')), parts along dimension 1
- sink_mass: float32 [14, 4096], P(None, ('doc', 'seq')), parts along dimension 1
- head_lse: float32 [28], P('doc'), parts along dimension 0
- head_sink: float32 [28], P('doc'), parts along dimension 0
There are 2 independent parts, one for each index of `doc`. A program takes and returns all parts, laid end to end along the dimension named above; each array names one. Nothing has to cross between parts.
Inputs may be any that keep to these rules, and one draw needn't show every extreme that they name: `sink_pos`: 4 distinct positions within the document's first 128 tokens; positions 0 and 127 are always among them. Positions from doc_length up to 2048 are padding.
All inputs are finite; a program needn't handle non-finite values.
Results may differ from a plain program's by a relative error of at most 0.009.
Values may be sent and summed in bfloat16 or wider, within the bound.
A program may use at most 64 MiB of HBM per device.

v0:
```python
import functools
import math

import jax
import jax.numpy as jnp
from jax import lax
from jax.experimental import pallas as pl
from jax.experimental.pallas import tpu as pltpu
from jax.sharding import PartitionSpec as P

HEAD_DIMENSION = 128
PLANE = 4
EXTRA = 16
MESH = pl.DeviceIdType.MESH
NEG = -1e30


def kernel(
    n, rows, heads, groups,
    len_ref, sink_ref, q_hbm, k_ref, v_ref,
    out_hbm, rl_ref, sm_ref, hd_ref,
    qb, kb, vb, vt, acc, mref, ob, stat_x, stat_tx, stat_rx,
    qsem, osem, ssem, rsem, tsem, usem,
):
    hd = HEAD_DIMENSION
    planes = n // PLANE
    span = PLANE * rows
    width = heads // groups
    me = lax.axis_index("seq")
    z = me // PLANE
    y = (me // 2) % 2
    c = me % 2
    scale = (hd ** -0.5) * math.log2(math.e)

    def block_id(p, yy, cc):
        return p * PLANE + yy * 2 + cc

    def block(ref, b):
        return ref.at[pl.ds(pl.multiple_of(b * rows, rows), rows)]

    ports = ((k_ref, kb, 0), (v_ref, vb, 1))

    def move(b, dev, slot, own=False):
        return [
            pltpu.make_async_remote_copy(
                src_ref=src if own else block(buf, b),
                dst_ref=block(buf, b),
                send_sem=ssem.at[kind, slot],
                recv_sem=rsem.at[kind, b],
                device_id={"seq": dev},
                device_id_type=MESH,
            )
            for src, buf, kind in ports
        ]

    def arrive(b, dev):
        return move(b, dev, 0)

    def slot_z(p):
        return p

    def slot_y(p):
        return planes + p

    def slot_c(p, k):
        return 2 * planes + 2 * p + k

    y_dev = block_id(z, 1 - y, c)
    c_dev = block_id(z, y, 1 - c)

    barrier = pltpu.get_barrier_semaphore()

    def greet(i, carry):
        pl.semaphore_signal(
            barrier, inc=1, device_id={"seq": (me + i) % n}, device_id_type=MESH
        )
        return carry

    lax.fori_loop(1, n, greet, 0)

    def q_copy(h):
        return pltpu.make_async_copy(
            q_hbm.at[:, pl.ds(h * hd, hd)], qb.at[pl.ds(h * rows, rows)], qsem.at[h]
        )

    for h in range(heads):
        q_copy(h).start()
    block(kb, me)[...] = k_ref[...]
    block(vb, me)[...] = v_ref[...]
    pl.semaphore_wait(barrier, n - 1)

    for copy in move(me, y_dev, slot_y(z), own=True):
        copy.start()
    for copy in move(me, c_dev, slot_c(z, 0), own=True):
        copy.start()

    def z_send(p):
        return move(me, block_id(p, y, c), slot_z(p), own=True)

    def send_up(i, carry):
        for copy in z_send(planes - 1 - i):
            copy.start()
        return carry

    lax.fori_loop(0, planes - 1 - z, send_up, 0)

    def take_z(p):
        b = block_id(p, y, c)
        for got, to_y, to_c in zip(
            arrive(b, y_dev), move(b, y_dev, slot_y(p)), move(b, c_dev, slot_c(p, 0))
        ):
            got.wait_recv()
            to_y.start()
            to_c.start()

    def take_y(p):
        b = block_id(p, 1 - y, c)
        for got, to_c in zip(arrive(b, y_dev), move(b, c_dev, slot_c(p, 1))):
            got.wait_recv()
            to_c.start()

    def take_c(p):
        for yy in (y, 1 - y):
            for got in arrive(block_id(p, yy, 1 - c), c_dev):
                got.wait_recv()

    def compute(p, g, first):
        base = pl.multiple_of(p * span, span)
        kp = kb[pl.ds(base, span), g * hd : (g + 1) * hd]
        vt[g, 0:hd, :] = vb[pl.ds(base, span), g * hd : (g + 1) * hd].T
        lane = lax.broadcasted_iota(jnp.int32, (EXTRA, span), 1) + base
        sub = lax.broadcasted_iota(jnp.int32, (EXTRA, span), 0)
        is_sink = lane == sink_ref[0]
        for i in range(1, sink_ref.shape[0]):
            is_sink = is_sink | (lane == sink_ref[i])
        marks = jnp.where(sub == 0, 1.0, jnp.where((sub == 1) & is_sink, 1.0, 0.0))
        vt[g, hd : hd + EXTRA, :] = marks.astype(jnp.bfloat16)
        vtg = vt[g]
        for h0 in range(0, width, 2):
            w = min(2, width - h0) * rows
            c0 = (g * width + h0) * rows
            cols = slice(c0, c0 + w)
            s = lax.dot_general(
                kp, qb[cols, :], (((1,), (1,)), ((), ())),
                preferred_element_type=jnp.float32,
            )
            if first:
                key_pos = base + lax.broadcasted_iota(jnp.int32, (span, w), 0)
                row = lax.broadcasted_iota(jnp.int32, (span, w), 1) % rows
                s = jnp.where(key_pos <= me * rows + row, s, NEG)
            top = jnp.max(s, axis=0, keepdims=True) * scale
            if first:
                new = top
            else:
                old = mref[:, cols]
                new = jnp.maximum(old, top)
            prob = jnp.exp2(s * scale - new).astype(jnp.bfloat16)
            part = jnp.dot(vtg, prob, preferred_element_type=jnp.float32)
            if first:
                acc[:, cols] = part
            else:
                acc[:, cols] = acc[:, cols] * jnp.exp2(old - new) + part
            mref[:, cols] = new

    take_y(z)
    for h in range(heads):
        q_copy(h).wait()
    take_c(z)

    def step(p, first):
        more = p > 0

        @pl.when(more)
        def _():
            take_z(p - 1)

        for g in range(groups):
            compute(p, g, first)
            if g == 0:
                @pl.when(more)
                def _():
                    take_y(p - 1)

        @pl.when(more)
        def _():
            take_c(p - 1)

    step(z, True)

    def body(t, carry):
        step(z - t, False)
        return carry

    lax.fori_loop(1, z + 1, body, 0)

    length = len_ref[0]
    live = (me * rows + lax.broadcasted_iota(jnp.int32, (1, rows), 1)) < length
    stat_x[...] = jnp.zeros_like(stat_x)
    for h in range(heads):
        cols = slice(h * rows, (h + 1) * rows)
        total = acc[hd : hd + 1, cols]
        lse = (mref[:, cols] + jnp.log2(total)) * math.log(2.0)
        lse = jnp.where(live, lse, 0.0)
        mass = jnp.where(live, acc[hd + 1 : hd + 2, cols] / total, 0.0)
        rl_ref[h : h + 1, :] = lse
        sm_ref[h : h + 1, :] = mass
        stat_x[h : h + 1, :] = lse
        stat_x[64 + h : 65 + h, :] = mass
    sums = lax.dot_general(
        jnp.ones((8, rows), jnp.float32), stat_x[...], (((1,), (1,)), ((), ())),
        precision=lax.Precision.HIGHEST, preferred_element_type=jnp.float32,
    )
    stat_tx[...] = sums[0:1]

    def stat_copy(i):
        dev = (me + i) % n
        return pltpu.make_async_remote_copy(
            src_ref=stat_tx,
            dst_ref=stat_rx.at[me],
            send_sem=tsem.at[i],
            recv_sem=usem.at[me],
            device_id={"seq": dev},
            device_id_type=MESH,
        )

    def stat_from(i):
        src = (me + i) % n
        return pltpu.make_async_remote_copy(
            src_ref=stat_tx,
            dst_ref=stat_rx.at[src],
            send_sem=tsem.at[i],
            recv_sem=usem.at[src],
            device_id={"seq": src},
            device_id_type=MESH,
        )

    def stat_start(i, carry):
        stat_copy(i).start()
        return carry

    lax.fori_loop(1, n, stat_start, 0)

    def o_copy(h):
        return pltpu.make_async_copy(
            ob.at[:, pl.ds(h * hd, hd)], out_hbm.at[:, pl.ds(h * hd, hd)], osem.at[h]
        )

    for h in range(heads):
        cols = slice(h * rows, (h + 1) * rows)
        inv = jnp.where(live, 1.0 / acc[hd : hd + 1, cols], 0.0)
        ob[:, h * hd : (h + 1) * hd] = (acc[0:hd, cols] * inv).T.astype(jnp.bfloat16)
        o_copy(h).start()

    def z_done(p, carry):
        for copy in z_send(p):
            copy.wait_send()
        return carry

    lax.fori_loop(z + 1, planes, z_done, 0)

    def yc_done(p, carry):
        for copy in move(block_id(p, y, c), y_dev, slot_y(p)):
            copy.wait_send()
        for k in range(2):
            for copy in move(block_id(p, y, c), c_dev, slot_c(p, k)):
                copy.wait_send()
        return carry

    lax.fori_loop(0, z + 1, yc_done, 0)

    def stat_wait(i, carry):
        stat_copy(i).wait_send()
        stat_from(i).wait_recv()
        return carry

    lax.fori_loop(1, n, stat_wait, 0)
    stat_rx[pl.ds(me, 1)] = stat_tx[...].reshape(1, 1, rows)
    hd_ref[...] = jnp.sum(stat_rx[...], axis=0) / length.astype(jnp.float32)
    for h in range(heads):
        o_copy(h).wait()


def body(n, queries, keys, values, doc_length, sink_pos):
    rows, qcols = queries.shape
    kcols = keys.shape[1]
    heads = qcols // HEAD_DIMENSION
    groups = kcols // HEAD_DIMENSION
    planes = n // PLANE
    f32, bf16 = jnp.float32, jnp.bfloat16
    smem = pl.BlockSpec(memory_space=pltpu.SMEM)
    vmem = pl.BlockSpec(memory_space=pltpu.VMEM)
    hbm = pl.BlockSpec(memory_space=pl.ANY)
    attended, row_lse, sink_mass, head = pl.pallas_call(
        functools.partial(kernel, n, rows, heads, groups),
        out_shape=(
            jax.ShapeDtypeStruct((rows, qcols), bf16),
            jax.ShapeDtypeStruct((heads, rows), f32),
            jax.ShapeDtypeStruct((heads, rows), f32),
            jax.ShapeDtypeStruct((1, 128), f32),
        ),
        in_specs=[smem, smem, hbm, vmem, vmem],
        out_specs=(hbm, vmem, vmem, vmem),
        scratch_shapes=[
            pltpu.VMEM((heads * rows, HEAD_DIMENSION), bf16),
            pltpu.VMEM((n * rows, kcols), bf16),
            pltpu.VMEM((n * rows, kcols), bf16),
            pltpu.VMEM((groups, HEAD_DIMENSION + EXTRA, PLANE * rows), bf16),
            pltpu.VMEM((HEAD_DIMENSION + EXTRA, heads * rows), f32),
            pltpu.VMEM((1, heads * rows), f32),
            pltpu.VMEM((rows, qcols), bf16),
            pltpu.VMEM((128, rows), f32),
            pltpu.VMEM((1, 128), f32),
            pltpu.VMEM((n, 1, 128), f32),
            pltpu.SemaphoreType.DMA((heads,)),
            pltpu.SemaphoreType.DMA((heads,)),
            pltpu.SemaphoreType.DMA((2, 4 * planes)),
            pltpu.SemaphoreType.DMA((2, n)),
            pltpu.SemaphoreType.DMA((n,)),
            pltpu.SemaphoreType.DMA((n,)),
        ],
        compiler_params=pltpu.CompilerParams(collective_id=0, has_side_effects=True),
    )(doc_length, sink_pos, queries, keys, values)
    return attended, row_lse, sink_mass, head[0, :heads], head[0, 64 : 64 + heads]


def solution(mesh):
    placed = (
        P(("doc", "seq"), None),
        P(("doc", "seq"), None),
        P(("doc", "seq"), None),
        P("doc"),
        P("doc"),
    )
    return jax.shard_map(
        functools.partial(body, mesh.shape["seq"]),
        mesh=mesh,
        in_specs=placed,
        out_specs=(
            P(("doc", "seq"), None),
            P(None, ("doc", "seq")),
            P(None, ("doc", "seq")),
            P("doc"),
            P("doc"),
        ),
        check_vma=False,
    )
```

profile of v0, /device:TPU:0, one launch (start us, length us, event | category | flops | bytes accessed | tf_op | source)
XLA Modules:
  0.0 47.0 jit_solution(3725245755518849647)
XLA Ops:
  1.3 41.4 %shard_map.92 = (bf16[128,1792]{1,0:T(8,128)(2,1)}, f32[14,128]{1,0:T(8,128)}, f32[14,128]{1,0:T(8,128)}, f32[1,128]{1,0:T(1,128)}) custom-call(s32[1]{0:T(128)S(6)} %copy.13.len_ref, s32[4]{0:T(128)} %sink_ref.1, bf16[128,1792]{1,0:T(8,128)(2,1)} %q_hbm.1, bf16[128,256]{1,0:T(8,128)(2,1)} %k_ref.1, bf16[128,256]{1,0:T(8,128)(2,1)} %v_ref.1), custom_call_target="tpu_custom_call" | custom-call | tf_op jit(solution)/shard_map/pallas_call | solution.py:293
  42.6 0.0 copy-start.2
  42.7 0.6 %copy-done.2 = f32[1,128]{1,0:T(1,128)S(1)} copy-done((f32[1,128]{1,0:T(1,128)S(1)}, f32[1,128]{1,0:T(1,128)}, u32[]{:S(2)}) %copy-start.2) | copy-done | bytes 536
  43.3 0.6 %slice_bitcast_fusion = (f32[14]{0:T(128)}, f32[14]{0:T(128)}) fusion(f32[1,128]{1,0:T(1,128)S(1)} %copy-done.2), kind=kLoop, calls=%fused_computation | loop fusion | bytes 224 | tf_op jit(solution)/shard_map/squeeze | solution.py:323
  43.9 0.0 copy-start.1
  43.9 1.8 %copy.14 = bf16[128,1792]{1,0:T(8,128)(2,1)} copy(bf16[128,1792]{1,0:T(8,128)(2,1)} %get-tuple-element.20) | data formatting | bytes 917504
  45.7 0.0 copy-done.1
  45.7 0.0 copy-start
  45.7 0.6 %copy.15 = f32[14,128]{1,0:T(8,128)} copy(f32[14,128]{1,0:T(8,128)S(1)} %copy-done.1) | data formatting | bytes 14336
  46.3 0.1 copy-done
  46.4 0.6 %copy.16 = f32[14,128]{1,0:T(8,128)} copy(f32[14,128]{1,0:T(8,128)S(1)} %copy-done) | data formatting | bytes 14336
Async XLA Ops:
  42.6 0.6 %copy-start.2 = (f32[1,128]{1,0:T(1,128)S(1)}, f32[1,128]{1,0:T(1,128)}, u32[]{:S(2)}) copy-start(f32[1,128]{1,0:T(1,128)} %get-tuple-element.12) | copy-start | bytes 1540
  43.9 1.8 %copy-start.1 = (f32[14,128]{1,0:T(8,128)S(1)}, f32[14,128]{1,0:T(8,128)}, u32[]{:S(2)}) copy-start(f32[14,128]{1,0:T(8,128)} %get-tuple-element.21) | copy-start | bytes 21508
  45.7 0.7 %copy-start = (f32[14,128]{1,0:T(8,128)S(1)}, f32[14,128]{1,0:T(8,128)}, u32[]{:S(2)}) copy-start(f32[14,128]{1,0:T(8,128)} %get-tuple-element.22) | copy-start | bytes 21508
where the time goes:
time: 47.2 us; the launch traced here: 47 us
  Pallas kernels  41.4 us (88%)
  local copies, waits for them, and re-layouts  4.34 us (9%)
  between operations  1.3 us (3%)
    pallas_call x1, Pallas kernels, body(): pl.pallas_call(functools.partial(kernel, n, rows, heads, groups), out_sha...  41.4 us
    unnamed x9, local copies, waits for them, and re-layouts  3.76 us

commit v1 on v0

--- a/solution.py
+++ b/solution.py
@@ -18,9 +18,9 @@
 def kernel(
     n, rows, heads, groups,
     len_ref, sink_ref, q_hbm, k_ref, v_ref,
-    out_hbm, rl_ref, sm_ref, hd_ref,
-    qb, kb, vb, vt, acc, mref, ob, stat_x, stat_tx, stat_rx,
-    qsem, osem, ssem, rsem, tsem, usem,
+    out_ref, rl_ref, sm_ref, hd_ref,
+    qb, kb, vb, vt, acc, mref, stat_x, stat_tx, stat_rx,
+    qsem, ssem, rsem, tsem, usem,
 ):
     hd = HEAD_DIMENSION
     planes = n // PLANE
@@ -89,27 +89,29 @@
     block(vb, me)[...] = v_ref[...]
     pl.semaphore_wait(barrier, n - 1)
 
+    up_dev = block_id(z + 1, y, c)
+    has_up = z + 1 < planes
+
+    @pl.when(has_up)
+    def _():
+        for copy in move(me, up_dev, slot_z(z), own=True):
+            copy.start()
+
     for copy in move(me, y_dev, slot_y(z), own=True):
         copy.start()
     for copy in move(me, c_dev, slot_c(z, 0), own=True):
         copy.start()
 
-    def z_send(p):
-        return move(me, block_id(p, y, c), slot_z(p), own=True)
-
-    def send_up(i, carry):
-        for copy in z_send(planes - 1 - i):
-            copy.start()
-        return carry
-
-    lax.fori_loop(0, planes - 1 - z, send_up, 0)
-
     def take_z(p):
         b = block_id(p, y, c)
-        for got, to_y, to_c in zip(
-            arrive(b, y_dev), move(b, y_dev, slot_y(p)), move(b, c_dev, slot_c(p, 0))
+        for got, to_z, to_y, to_c in zip(
+            arrive(b, y_dev),
+            move(b, up_dev, slot_z(p)),
+            move(b, y_dev, slot_y(p)),
+            move(b, c_dev, slot_c(p, 0)),
         ):
             got.wait_recv()
+            pl.when(has_up)(to_z.start)
             to_y.start()
             to_c.start()
 
@@ -136,10 +138,14 @@
         marks = jnp.where(sub == 0, 1.0, jnp.where((sub == 1) & is_sink, 1.0, 0.0))
         vt[g, hd : hd + EXTRA, :] = marks.astype(jnp.bfloat16)
         vtg = vt[g]
+        pieces = []
         for h0 in range(0, width, 2):
             w = min(2, width - h0) * rows
             c0 = (g * width + h0) * rows
-            cols = slice(c0, c0 + w)
+            pieces.append((w, slice(c0, c0 + w)))
+
+        def scores(piece):
+            w, cols = piece
             s = lax.dot_general(
                 kp, qb[cols, :], (((1,), (1,)), ((), ())),
                 preferred_element_type=jnp.float32,
@@ -148,6 +154,13 @@
                 key_pos = base + lax.broadcasted_iota(jnp.int32, (span, w), 0)
                 row = lax.broadcasted_iota(jnp.int32, (span, w), 1) % rows
                 s = jnp.where(key_pos <= me * rows + row, s, NEG)
+            return s
+
+        ahead = scores(pieces[0])
+        for j, (w, cols) in enumerate(pieces):
+            s = ahead
+            if j + 1 < len(pieces):
+                ahead = scores(pieces[j + 1])
             top = jnp.max(s, axis=0, keepdims=True) * scale
             if first:
                 new = top
@@ -162,36 +175,38 @@
                 acc[:, cols] = acc[:, cols] * jnp.exp2(old - new) + part
             mref[:, cols] = new
 
+    @pl.when(z > 0)
+    def _():
+        take_z(z - 1)
+
     take_y(z)
     for h in range(heads):
         q_copy(h).wait()
     take_c(z)
 
     def step(p, first):
-        more = p > 0
-
-        @pl.when(more)
-        def _():
-            take_z(p - 1)
-
         for g in range(groups):
             compute(p, g, first)
             if g == 0:
-                @pl.when(more)
+                @pl.when(p > 1)
+                def _():
+                    take_z(p - 2)
+
+                @pl.when(p > 0)
                 def _():
                     take_y(p - 1)
 
-        @pl.when(more)
+        @pl.when(p > 0)
         def _():
             take_c(p - 1)
 
     step(z, True)
 
-    def body(t, carry):
+    def later(t, carry):
         step(z - t, False)
         return carry
 
-    lax.fori_loop(1, z + 1, body, 0)
+    lax.fori_loop(1, z + 1, later, 0)
 
     length = len_ref[0]
     live = (me * rows + lax.broadcasted_iota(jnp.int32, (1, rows), 1)) < length
@@ -240,25 +255,17 @@
 
     lax.fori_loop(1, n, stat_start, 0)
 
-    def o_copy(h):
-        return pltpu.make_async_copy(
-            ob.at[:, pl.ds(h * hd, hd)], out_hbm.at[:, pl.ds(h * hd, hd)], osem.at[h]
-        )
-
     for h in range(heads):
         cols = slice(h * rows, (h + 1) * rows)
         inv = jnp.where(live, 1.0 / acc[hd : hd + 1, cols], 0.0)
-        ob[:, h * hd : (h + 1) * hd] = (acc[0:hd, cols] * inv).T.astype(jnp.bfloat16)
-        o_copy(h).start()
-
-    def z_done(p, carry):
-        for copy in z_send(p):
-            copy.wait_send()
-        return carry
-
-    lax.fori_loop(z + 1, planes, z_done, 0)
+        out_ref[:, h * hd : (h + 1) * hd] = (acc[0:hd, cols] * inv).T.astype(jnp.bfloat16)
 
     def yc_done(p, carry):
+        @pl.when(has_up)
+        def _():
+            for copy in move(block_id(p, y, c), up_dev, slot_z(p)):
+                copy.wait_send()
+
         for copy in move(block_id(p, y, c), y_dev, slot_y(p)):
             copy.wait_send()
         for k in range(2):
@@ -276,8 +283,6 @@
     lax.fori_loop(1, n, stat_wait, 0)
     stat_rx[pl.ds(me, 1)] = stat_tx[...].reshape(1, 1, rows)
     hd_ref[...] = jnp.sum(stat_rx[...], axis=0) / length.astype(jnp.float32)
-    for h in range(heads):
-        o_copy(h).wait()
 
 
 def body(n, queries, keys, values, doc_length, sink_pos):
@@ -299,7 +304,7 @@
             jax.ShapeDtypeStruct((1, 128), f32),
         ),
         in_specs=[smem, smem, hbm, vmem, vmem],
-        out_specs=(hbm, vmem, vmem, vmem),
+        out_specs=(vmem, vmem, vmem, vmem),
         scratch_shapes=[
             pltpu.VMEM((heads * rows, HEAD_DIMENSION), bf16),
             pltpu.VMEM((n * rows, kcols), bf16),
@@ -307,18 +312,17 @@
             pltpu.VMEM((groups, HEAD_DIMENSION + EXTRA, PLANE * rows), bf16),
             pltpu.VMEM((HEAD_DIMENSION + EXTRA, heads * rows), f32),
             pltpu.VMEM((1, heads * rows), f32),
-            pltpu.VMEM((rows, qcols), bf16),
             pltpu.VMEM((128, rows), f32),
             pltpu.VMEM((1, 128), f32),
             pltpu.VMEM((n, 1, 128), f32),
-            pltpu.SemaphoreType.DMA((heads,)),
             pltpu.SemaphoreType.DMA((heads,)),
             pltpu.SemaphoreType.DMA((2, 4 * planes)),
             pltpu.SemaphoreType.DMA((2, n)),
             pltpu.SemaphoreType.DMA((n,)),
             pltpu.SemaphoreType.DMA((n,)),
         ],
-        compiler_params=pltpu.CompilerParams(collective_id=0, has_side_effects=True),
+        compiler_params=pltpu.CompilerParams(collective_id=0, has_side_effects=True, vmem_limit_bytes=(12 + n // 4) << 20
+        ),
     )(doc_length, sink_pos, queries, keys, values)
     return attended, row_lse, sink_mass, head[0, :heads], head[0, 64 : 64 + heads]
 

time: 47.2 us -> 36.9 us (0.78)
  Pallas kernels: 41.4 us -> 30.1 us
  local copies, waits for them, and re-layouts: 4.34 us -> 5.24 us
    pallas_call x1, Pallas kernels: 41.4 us -> 30.1 us  [body(): pl.pallas_call(functools.partial(kernel, n, rows, heads, groups), out_sha...]
    unnamed x9 -> x11, local copies, waits for them, and re-layouts: 3.76 us -> 4.66 us
where the time goes in v1:
time: 36.9 us; the launch traced here: 36.7 us
  Pallas kernels  30.1 us (82%)
  local copies, waits for them, and re-layouts  5.24 us (14%)
  between operations  1.33 us (4%)
    pallas_call x1, Pallas kernels, body(): pl.pallas_call(functools.partial(kernel, n, rows, heads, groups), out_sha...  30.1 us
    unnamed x11, local copies, waits for them, and re-layouts  4.66 us

profile of v1, /device:TPU:0, one launch (start us, length us, event | category | flops | bytes accessed | tf_op | source)
XLA Modules:
  0.0 36.7 jit_solution(12533054563046394884)
XLA Ops:
  0.6 0.0 copy-start.3
  1.3 0.0 copy-done.3
  1.3 0.0 copy-start
  1.3 1.0 %copy-done = bf16[128,1792]{1,0:T(8,128)(2,1)S(1)} copy-done((bf16[128,1792]{1,0:T(8,128)(2,1)S(1)}, bf16[128,1792]{1,0:T(8,128)(2,1)}, u32[]{:S(2)}) %copy-start) | copy-done | bytes 458776
  2.3 0.0 copy-start.1
  2.3 0.8 %copy-done.1 = bf16[128,256]{1,0:T(8,128)(2,1)S(1)} copy-done((bf16[128,256]{1,0:T(8,128)(2,1)S(1)}, bf16[128,256]{1,0:T(8,128)(2,1)}, u32[]{:S(2)}) %copy-start.1) | copy-done | bytes 65560
  3.2 0.0 copy-start.2
  3.2 0.8 %copy-done.2 = bf16[128,256]{1,0:T(8,128)(2,1)S(1)} copy-done((bf16[128,256]{1,0:T(8,128)(2,1)S(1)}, bf16[128,256]{1,0:T(8,128)(2,1)}, u32[]{:S(2)}) %copy-start.2) | copy-done | bytes 65560
  4.0 30.1 %shard_map.92 = (bf16[128,1792]{1,0:T(8,128)(2,1)S(1)}, f32[14,128]{1,0:T(8,128)S(1)}, f32[14,128]{1,0:T(8,128)S(1)}, f32[1,128]{1,0:T(1,128)S(1)}) custom-call(s32[1]{0:T(128)S(6)} %copy.13.len_ref, s32[4]{0:T(128)S(1)} %copy-done.3, bf16[128,1792]{1,0:T(8,128)(2,1)S(1)} %copy-done, bf16[128,256]{1,0:T(8,128)(2,1)S(1)} %copy-done.1, ...), custom_call_target="tpu_custom_call" | custom-call | tf_op jit(solution)/shard_map/pallas_call | solution.py:298
  34.1 0.6 %slice_bitcast_fusion = (f32[14]{0:T(128)}, f32[14]{0:T(128)}) fusion(f32[1,128]{1,0:T(1,128)S(1)} %get-tuple-element.12), kind=kLoop, calls=%fused_computation | loop fusion | bytes 224 | tf_op jit(solution)/shard_map/squeeze | solution.py:327
  34.7 0.8 %copy.14 = bf16[128,1792]{1,0:T(8,128)(2,1)} copy(bf16[128,1792]{1,0:T(8,128)(2,1)S(1)} %get-tuple-element.20) | data formatting | bytes 917504
  35.5 0.6 %copy.15 = f32[14,128]{1,0:T(8,128)} copy(f32[14,128]{1,0:T(8,128)S(1)} %get-tuple-element.21) | data formatting | bytes 14336
  36.1 0.6 %copy.16 = f32[14,128]{1,0:T(8,128)} copy(f32[14,128]{1,0:T(8,128)S(1)} %get-tuple-element.22) | data formatting | bytes 14336
Async XLA Ops:
  0.6 0.7 %copy-start.3 = (s32[4]{0:T(128)S(1)}, s32[4]{0:T(128)}, u32[]{:S(2)}) copy-start(s32[4]{0:T(128)} %sink_ref.1) | copy-start | bytes 52
  1.3 1.0 %copy-start = (bf16[128,1792]{1,0:T(8,128)(2,1)S(1)}, bf16[128,1792]{1,0:T(8,128)(2,1)}, u32[]{:S(2)}) copy-start(bf16[128,1792]{1,0:T(8,128)(2,1)} %q_hbm.1) | copy-start | bytes 1376260
  2.3 0.8 %copy-start.1 = (bf16[128,256]{1,0:T(8,128)(2,1)S(1)}, bf16[128,256]{1,0:T(8,128)(2,1)}, u32[]{:S(2)}) copy-start(bf16[128,256]{1,0:T(8,128)(2,1)} %k_ref.1) | copy-start | bytes 196612
  3.2 0.8 %copy-start.2 = (bf16[128,256]{1,0:T(8,128)(2,1)S(1)}, bf16[128,256]{1,0:T(8,128)(2,1)}, u32[]{:S(2)}) copy-start(bf16[128,256]{1,0:T(8,128)(2,1)} %v_ref.1) | copy-start | bytes 196612

commit v2 on v1

--- a/solution.py
+++ b/solution.py
@@ -10,6 +10,7 @@
 
 HEAD_DIMENSION = 128
 PLANE = 4
+PARTS = 2
 EXTRA = 16
 MESH = pl.DeviceIdType.MESH
 NEG = -1e30
@@ -18,13 +19,13 @@
 def kernel(
     n, rows, heads, groups,
     len_ref, sink_ref, q_hbm, k_ref, v_ref,
-    out_ref, rl_ref, sm_ref, hd_ref,
+    out_ref, st_ref,
     qb, kb, vb, vt, acc, mref, stat_x, stat_tx, stat_rx,
-    qsem, ssem, rsem, tsem, usem,
+    qsem, ssem, rsem, lsem, tsem, usem,
 ):
     hd = HEAD_DIMENSION
     planes = n // PLANE
-    span = PLANE * rows
+    span = 2 * rows
     width = heads // groups
     me = lax.axis_index("seq")
     z = me // PLANE
@@ -38,19 +39,23 @@
     def block(ref, b):
         return ref.at[pl.ds(pl.multiple_of(b * rows, rows), rows)]
 
-    ports = ((k_ref, kb, 0), (v_ref, vb, 1))
-
-    def move(b, dev, slot, own=False):
+    half = rows // PARTS
+
+    def piece(buf, b, part):
+        return buf.at[pl.ds(pl.multiple_of(b * rows + part * half, half), half)]
+
+    def move(b, dev, slot):
         return [
             pltpu.make_async_remote_copy(
-                src_ref=src if own else block(buf, b),
-                dst_ref=block(buf, b),
-                send_sem=ssem.at[kind, slot],
-                recv_sem=rsem.at[kind, b],
+                src_ref=piece(buf, b, part),
+                dst_ref=piece(buf, b, part),
+                send_sem=ssem.at[kind * PARTS + part, slot],
+                recv_sem=rsem.at[kind * PARTS + part, b],
                 device_id={"seq": dev},
                 device_id_type=MESH,
             )
-            for src, buf, kind in ports
+            for kind, buf in enumerate((kb, vb))
+            for part in range(PARTS)
         ]
 
     def arrive(b, dev):
@@ -68,6 +73,12 @@
     y_dev = block_id(z, 1 - y, c)
     c_dev = block_id(z, y, 1 - c)
 
+    loads = [
+        pltpu.make_async_copy(src, block(buf, me), lsem.at[i])
+        for i, (src, buf) in enumerate(((k_ref, kb), (v_ref, vb)))
+    ]
+    for load in loads:
+        load.start()
     barrier = pltpu.get_barrier_semaphore()
 
     def greet(i, carry):
@@ -85,8 +96,8 @@
 
     for h in range(heads):
         q_copy(h).start()
-    block(kb, me)[...] = k_ref[...]
-    block(vb, me)[...] = v_ref[...]
+    for load in loads:
+        load.wait()
     pl.semaphore_wait(barrier, n - 1)
 
     up_dev = block_id(z + 1, y, c)
@@ -94,12 +105,12 @@
 
     @pl.when(has_up)
     def _():
-        for copy in move(me, up_dev, slot_z(z), own=True):
+        for copy in move(me, up_dev, slot_z(z)):
             copy.start()
 
-    for copy in move(me, y_dev, slot_y(z), own=True):
+    for copy in move(me, y_dev, slot_y(z)):
         copy.start()
-    for copy in move(me, c_dev, slot_c(z, 0), own=True):
+    for copy in move(me, c_dev, slot_c(z, 0)):
         copy.start()
 
     def take_z(p):
@@ -121,13 +132,12 @@
             got.wait_recv()
             to_c.start()
 
-    def take_c(p):
-        for yy in (y, 1 - y):
-            for got in arrive(block_id(p, yy, 1 - c), c_dev):
-                got.wait_recv()
-
-    def compute(p, g, first):
-        base = pl.multiple_of(p * span, span)
+    def take_c(p, yy):
+        for got in arrive(block_id(p, yy, 1 - c), c_dev):
+            got.wait_recv()
+
+    def compute(p, yy, g, first=False, masked=False):
+        base = pl.multiple_of((p * 2 + yy) * span, span)
         kp = kb[pl.ds(base, span), g * hd : (g + 1) * hd]
         vt[g, 0:hd, :] = vb[pl.ds(base, span), g * hd : (g + 1) * hd].T
         lane = lax.broadcasted_iota(jnp.int32, (EXTRA, span), 1) + base
@@ -150,7 +160,7 @@
                 kp, qb[cols, :], (((1,), (1,)), ((), ())),
                 preferred_element_type=jnp.float32,
             )
-            if first:
+            if masked:
                 key_pos = base + lax.broadcasted_iota(jnp.int32, (span, w), 0)
                 row = lax.broadcasted_iota(jnp.int32, (span, w), 1) % rows
                 s = jnp.where(key_pos <= me * rows + row, s, NEG)
@@ -175,30 +185,39 @@
                 acc[:, cols] = acc[:, cols] * jnp.exp2(old - new) + part
             mref[:, cols] = new
 
+    for h in range(heads):
+        q_copy(h).wait()
+    take_c(z, y)
+    for g in range(groups):
+        compute(z, y, g, first=True, masked=True)
+
     @pl.when(z > 0)
     def _():
         take_z(z - 1)
 
     take_y(z)
-    for h in range(heads):
-        q_copy(h).wait()
-    take_c(z)
-
-    def step(p, first):
-        for g in range(groups):
-            compute(p, g, first)
-            if g == 0:
-                @pl.when(p > 1)
-                def _():
-                    take_z(p - 2)
-
-                @pl.when(p > 0)
-                def _():
-                    take_y(p - 1)
+
+    def step(p, masked):
+        @pl.when(p > 1)
+        def _():
+            take_z(p - 2)
+
+        take_c(p, 1 - y)
+        if masked:
+            @pl.when(y == 1)
+            def _():
+                for g in range(groups):
+                    compute(p, 1 - y, g, masked=True)
+        else:
+            for g in range(groups):
+                compute(p, 1 - y, g)
 
         @pl.when(p > 0)
         def _():
-            take_c(p - 1)
+            take_y(p - 1)
+            take_c(p - 1, y)
+            for g in range(groups):
+                compute(p - 1, y, g)
 
     step(z, True)
 
@@ -217,8 +236,8 @@
         lse = (mref[:, cols] + jnp.log2(total)) * math.log(2.0)
         lse = jnp.where(live, lse, 0.0)
         mass = jnp.where(live, acc[hd + 1 : hd + 2, cols] / total, 0.0)
-        rl_ref[h : h + 1, :] = lse
-        sm_ref[h : h + 1, :] = mass
+        st_ref[h : h + 1, :] = lse
+        st_ref[32 + h : 33 + h, :] = mass
         stat_x[h : h + 1, :] = lse
         stat_x[64 + h : 65 + h, :] = mass
     sums = lax.dot_general(
@@ -282,7 +301,17 @@
 
     lax.fori_loop(1, n, stat_wait, 0)
     stat_rx[pl.ds(me, 1)] = stat_tx[...].reshape(1, 1, rows)
-    hd_ref[...] = jnp.sum(stat_rx[...], axis=0) / length.astype(jnp.float32)
+    st_ref[64:65, :] = jnp.sum(stat_rx[...], axis=0) / length.astype(jnp.float32)
+
+
+def emit(heads, att_ref, st_ref, out_hbm, rl_ref, sm_ref, hl_ref, hs_ref, sem):
+    copy = pltpu.make_async_copy(att_ref, out_hbm, sem)
+    copy.start()
+    rl_ref[...] = st_ref[0:heads]
+    sm_ref[...] = st_ref[32 : 32 + heads]
+    hl_ref[...] = st_ref[64, 0:heads]
+    hs_ref[...] = st_ref[64, 64 : 64 + heads]
+    copy.wait()
 
 
 def body(n, queries, keys, values, doc_length, sink_pos):
@@ -294,37 +323,49 @@
     f32, bf16 = jnp.float32, jnp.bfloat16
     smem = pl.BlockSpec(memory_space=pltpu.SMEM)
     vmem = pl.BlockSpec(memory_space=pltpu.VMEM)
-    hbm = pl.BlockSpec(memory_space=pl.ANY)
-    attended, row_lse, sink_mass, head = pl.pallas_call(
+    hbm = pl.BlockSpec(memory_space=pltpu.HBM)
+    attended, stats = pl.pallas_call(
         functools.partial(kernel, n, rows, heads, groups),
         out_shape=(
             jax.ShapeDtypeStruct((rows, qcols), bf16),
-            jax.ShapeDtypeStruct((heads, rows), f32),
-            jax.ShapeDtypeStruct((heads, rows), f32),
-            jax.ShapeDtypeStruct((1, 128), f32),
+            jax.ShapeDtypeStruct((72, rows), f32),
         ),
-        in_specs=[smem, smem, hbm, vmem, vmem],
-        out_specs=(vmem, vmem, vmem, vmem),
+        in_specs=[smem, smem, hbm, hbm, hbm],
+        out_specs=(vmem, vmem),
         scratch_shapes=[
             pltpu.VMEM((heads * rows, HEAD_DIMENSION), bf16),
             pltpu.VMEM((n * rows, kcols), bf16),
             pltpu.VMEM((n * rows, kcols), bf16),
-            pltpu.VMEM((groups, HEAD_DIMENSION + EXTRA, PLANE * rows), bf16),
+            pltpu.VMEM((groups, HEAD_DIMENSION + EXTRA, 2 * rows), bf16),
             pltpu.VMEM((HEAD_DIMENSION + EXTRA, heads * rows), f32),
             pltpu.VMEM((1, heads * rows), f32),
             pltpu.VMEM((128, rows), f32),
             pltpu.VMEM((1, 128), f32),
             pltpu.VMEM((n, 1, 128), f32),
             pltpu.SemaphoreType.DMA((heads,)),
-            pltpu.SemaphoreType.DMA((2, 4 * planes)),
-            pltpu.SemaphoreType.DMA((2, n)),
+            pltpu.SemaphoreType.DMA((2 * PARTS, 4 * planes)),
+            pltpu.SemaphoreType.DMA((2 * PARTS, n)),
+            pltpu.SemaphoreType.DMA((2,)),
             pltpu.SemaphoreType.DMA((n,)),
             pltpu.SemaphoreType.DMA((n,)),
         ],
-        compiler_params=pltpu.CompilerParams(collective_id=0, has_side_effects=True, vmem_limit_bytes=(12 + n // 4) << 20
+        compiler_params=pltpu.CompilerParams(collective_id=0, has_side_effects=True, vmem_limit_bytes=62 << 20
         ),
     )(doc_length, sink_pos, queries, keys, values)
-    return attended, row_lse, sink_mass, head[0, :heads], head[0, 64 : 64 + heads]
+    return pl.pallas_call(
+        functools.partial(emit, heads),
+        out_shape=(
+            jax.ShapeDtypeStruct((rows, qcols), bf16),
+            jax.ShapeDtypeStruct((heads, rows), f32),
+            jax.ShapeDtypeStruct((heads, rows), f32),
+            jax.ShapeDtypeStruct((heads,), f32),
+            jax.ShapeDtypeStruct((heads,), f32),
+        ),
+        in_specs=[vmem, vmem],
+        out_specs=(hbm, vmem, vmem, vmem, vmem),
+        scratch_shapes=[pltpu.SemaphoreType.DMA],
+        compiler_params=pltpu.CompilerParams(vmem_limit_bytes=4 << 20),
+    )(attended, stats)
 
 
 def solution(mesh):

time: 36.9 us -> 34.4 us (0.932)
  local copies, waits for them, and re-layouts: 5.24 us -> 1.78 us
  Pallas kernels: 30.1 us -> 31.1 us
    unnamed x11 -> x4, local copies, waits for them, and re-layouts: 4.66 us -> 1.78 us
    pallas_call x0 -> x1, Pallas kernels: none -> 1.38 us  [body(): pl.pallas_call(functools.partial(emit, heads), out_shape=(jax.ShapeDtypeS...]
    squeeze x1 -> x0, local copies, waits for them, and re-layouts: 0.58 us -> none  [body(): head[0, 64:64 + heads]]
    pallas_call x1, Pallas kernels: 30.1 us -> 29.7 us  [body(): pl.pallas_call(functools.partial(kernel, n, rows, heads, groups), out_sha...]
where the time goes in v2:
time: 34.4 us; the launch traced here: 34.1 us
  Pallas kernels  31.1 us (90%)
  local copies, waits for them, and re-layouts  1.78 us (5%)
  between operations  1.3 us (4%)
    pallas_call x1, Pallas kernels, body(): pl.pallas_call(functools.partial(kernel, n, rows, heads, groups), out_sha...  29.7 us
    unnamed x4, local copies, waits for them, and re-layouts  1.78 us
    pallas_call x1, Pallas kernels, body(): pl.pallas_call(functools.partial(emit, heads), out_shape=(jax.ShapeDtypeS...  1.38 us

profile of v2, /device:TPU:0, one launch (start us, length us, event | category | flops | bytes accessed | tf_op | source)
XLA Modules:
  0.0 34.1 jit_solution(3352383704033239873)
XLA Ops:
  1.3 29.7 %shard_map.92 = (bf16[128,1792]{1,0:T(8,128)(2,1)}, f32[72,128]{1,0:T(8,128)}) custom-call(s32[1]{0:T(128)S(6)} %copy.10.len_ref, s32[4]{0:T(128)} %sink_ref.1, bf16[128,1792]{1,0:T(8,128)(2,1)} %q_hbm.1, bf16[128,256]{1,0:T(8,128)(2,1)} %k_ref.1, bf16[128,256]{1,0:T(8,128)(2,1)} %v_ref.1), custom_call_target="tpu_custom_call" | custom-call | tf_op jit(solution)/shard_map/pallas_call | solution.py:327
  31.0 0.0 copy-start
  31.0 1.0 %copy-done = bf16[128,1792]{1,0:T(8,128)(2,1)S(1)} copy-done((bf16[128,1792]{1,0:T(8,128)(2,1)S(1)}, bf16[128,1792]{1,0:T(8,128)(2,1)}, u32[]{:S(2)}) %copy-start) | copy-done | bytes 458776
  32.0 0.0 copy-start.1
  32.0 0.8 %copy-done.1 = f32[72,128]{1,0:T(8,128)S(1)} copy-done((f32[72,128]{1,0:T(8,128)S(1)}, f32[72,128]{1,0:T(8,128)}, u32[]{:S(2)}) %copy-start.1) | copy-done | bytes 36888
  32.8 1.4 %shard_map.93 = (bf16[128,1792]{1,0:T(8,128)(2,1)}, f32[14,128]{1,0:T(8,128)}, f32[14,128]{1,0:T(8,128)}, f32[14]{0:T(128)}, f32[14]{0:T(128)}) custom-call(bf16[128,1792]{1,0:T(8,128)(2,1)S(1)} %copy-done, f32[72,128]{1,0:T(8,128)S(1)} %copy-done.1), custom_call_target="tpu_custom_call" | custom-call | tf_op jit(solution)/shard_map/pallas_call | solution.py:355
Async XLA Ops:
  31.0 1.0 %copy-start = (bf16[128,1792]{1,0:T(8,128)(2,1)S(1)}, bf16[128,1792]{1,0:T(8,128)(2,1)}, u32[]{:S(2)}) copy-start(bf16[128,1792]{1,0:T(8,128)(2,1)} %get-tuple-element.7.att_ref) | copy-start | bytes 1376260
  32.0 0.8 %copy-start.1 = (f32[72,128]{1,0:T(8,128)S(1)}, f32[72,128]{1,0:T(8,128)}, u32[]{:S(2)}) copy-start(f32[72,128]{1,0:T(8,128)} %get-tuple-element.8.st_ref) | copy-start | bytes 110596
